TPU v7x, 32 devices: a whole 2x2x4 slice. The times are simulated.
32 devices in a mesh: task: 8 (over z, core), tp: 4 (over y, x).
Axes of the slice: x: 2, y: 2, z: 4, core: 2. Of those that a mesh axis runs over, the one named last changes fastest.
Arguments:
- support_x: bfloat16 [8, 384, 3584], P('task'), may hold values from -6 to 6
- adapter_a: bfloat16 [8, 3584, 64], P('task'), may hold values from -0.09375 to 0.09375
- gate_pre: bfloat16 [8, 384, 10240], P('task', None, 'tp'), may hold values from -6 to 6
- lengths: int32 [8], P('task'), may hold values from 128 to 384, as said below
- damping: float32 [8], P('task'), may hold values from 0.03 to 0.3
- down_w: bfloat16 [10240, 3584], P('tp', 'task'), may hold values from -0.0625 to 0.0625
- grad_b: float32 [8, 64, 10240], P('task', None, 'tp'), may hold values from -6 to 6
Outputs:
- solution: float32 [8, 64, 10240], P('task', None, 'tp')
- residual: float32 [8, 64, 10240], P('task', None, 'tp')
Inputs may be any that keep to these rules, and one draw needn't show every extreme that they name: `lengths`: each a multiple of 128; some task has exactly 384.
All inputs are finite; a program needn't handle non-finite values.
Results may differ from a plain program's by a relative error of at most 0.033.
Values may be sent and summed in bfloat16 or wider, within the bound.
A program may use at most 64 MiB of HBM per device.

v0:
```python
import jax
import jax.numpy as jnp
from jax import lax
from jax.sharding import PartitionSpec as P

ITERS = 2


def shards(support_x, adapter_a, gate_pre, lengths, damping, down_w, grad_b):
    down_full = lax.all_gather(down_w, "task", axis=1, tiled=True)
    features = jnp.dot(support_x[0], adapter_a[0], preferred_element_type=jnp.float32).astype(
        jnp.bfloat16
    )
    positions = lax.broadcasted_iota(jnp.int32, (gate_pre.shape[1], 1), 0)
    gated = jnp.where(
        positions < lengths[0], jax.nn.silu(gate_pre[0].astype(jnp.float32)), 0.0
    ).astype(jnp.bfloat16)
    tokens_live = lengths[0].astype(jnp.float32)
    damping_rate = damping[0]

    def transposed(mixed_rows):
        return lax.dot_general(
            mixed_rows, down_full, (((1,), (1,)), ((), ())), preferred_element_type=jnp.float32
        )

    def apply(vector):
        inner = jnp.dot(features, vector.astype(jnp.bfloat16), preferred_element_type=jnp.float32)
        active = (gated * inner).astype(jnp.bfloat16)
        partial_sum = jnp.dot(active, down_full, preferred_element_type=jnp.float32)
        mixed = lax.psum(partial_sum.astype(jnp.bfloat16), "tp")
        second = (gated * transposed(mixed)).astype(jnp.bfloat16)
        product = lax.dot_general(
            features, second, (((0,), (0,)), ((), ())), preferred_element_type=jnp.float32
        )
        return product / tokens_live + damping_rate * vector

    def paired_sums(vector, image):
        return lax.psum((jnp.sum(vector * vector), jnp.sum(vector * image)), "tp")

    target = grad_b[0]
    solution = jnp.zeros_like(target)
    residual = target
    image = apply(residual)
    norm_now, product = paired_sums(residual, image)
    alpha = norm_now / product
    direction, along = (residual, image)
    for step in range(ITERS):
        solution = solution + alpha * direction
        residual = residual - alpha * along
        if step + 1 < ITERS:
            image = apply(residual)
            norm_next, product = paired_sums(residual, image)
            ratio = norm_next / norm_now
            alpha = norm_next / (product - ratio * norm_next / alpha)
            direction = residual + ratio * direction
            along = image + ratio * along
            norm_now = norm_next
    return (solution[None], residual[None])


def solution(mesh):
    in_specs = (
        P("task", None, None),
        P("task", None, None),
        P("task", None, "tp"),
        P("task"),
        P("task"),
        P("tp", "task"),
        P("task", None, "tp"),
    )
    out_specs = (P("task", None, "tp"), P("task", None, "tp"))
    return jax.shard_map(shards, mesh=mesh, in_specs=in_specs, out_specs=out_specs, check_vma=False)
```

profile of v0, /device:TPU:0, one launch (start us, length us, event | category | flops | bytes accessed | tf_op | source)
XLA Modules:
  0.0 429.8 jit_solution(7831728093009791851)
XLA Ops:
  7.2 0.0 copy-start
  7.2 0.0 copy-start.1
  7.2 0.0 all-gather.2.cloned.1.call-start
  7.2 0.7 all-gather.2.cloned.1.call-update
  7.9 0.0 all-reduce.5.cloned.1.call-start
  8.9 0.1 copy-done
  8.9 2.0 fusion.13
  10.9 165.4 %all-gather.2.cloned.1.call-done = bf16[2560,3584]{0,1:T(8,128)(2,1)} async-done(((bf16[2560,448]{0,1:T(8,128)(2,1)}), bf16[2560,3584]{0,1:T(8,128)(2,1)}) %all-gather.2.cloned.1.call-update) | async-done | bytes 18350096 | tf_op jit(solution)/shard_map/all_gather | solution.py:10
  176.4 0.0 copy-done.1
  176.4 14.4 %convolution_convert_fusion.1 = bf16[384,3584]{1,0:T(8,128)(2,1)} fusion(bf16[2560,3584]{0,1:T(8,128)(2,1)} %all-gather.2.cloned.1.call-done, bf16[384,64]{0,1:T(8,128)(2,1)S(1)} %fusion.13, f32[1,64,2560]{2,1,0:T(8,128)S(1)} %copy-done.1, bf16[1,384,2560]{2,1,0:T(8,128)(2,1)} %param.9, pred[384]{0:T(512)(128)(4,1)S(1)} %iota_compare_fusion), kind=kOutput, calls=%fused_computation.5 | convolution fusion | flops 7183466496 | bytes 23773568 | tf_op jit(solution)/shard_map/dot_general | solution.py:29
  190.8 0.0 all-reduce.5.cloned.1.call-update
  190.8 0.0 all-reduce.7.cloned.1.call-start
  191.5 78.1 %all-reduce.5.cloned.1.call-done = bf16[384,3584]{1,0:T(8,128)(2,1)} async-done(((bf16[384,3584]{1,0:T(8,128)(2,1)}), bf16[384,3584]{1,0:T(8,128)(2,1)}) %all-reduce.5.cloned.1.call-update) | async-done | bytes 2752528 | tf_op jit(solution)/shard_map/psum | solution.py:30
  269.5 14.3 %fusion.17 = (f32[]{:T(128)}, f32[]{:T(128)}, f32[64,2560]{1,0:T(8,128)}) fusion(f32[1,64,2560]{2,1,0:T(8,128)S(1)} %copy-done.1, f32[]{:T(128)} %bitcast.71, f32[]{:T(128)S(6)} %convert_element_type.54, bf16[384,64]{0,1:T(8,128)(2,1)S(1)} %fusion.13, bf16[384,3584]{1,0:T(8,128)(2,1)} %all-reduce.5.cloned.1.call-done, ...), kind=kOutput, calls=%fused_computation.32 | convolution fusion | flops 7183237120 | bytes 24428944 | tf_op jit(solution)/shard_map/dot_general | solution.py:32
  283.9 9.7 %all-reduce.1 = (f32[]{:T(128)}, f32[]{:T(128)}) all-reduce(f32[]{:T(128)} %get-tuple-element.5, f32[]{:T(128)} %get-tuple-element.4), channel_id=1, replica_groups=mesh['task'=8,'tp'=4] {'tp'}, use_global_device_ids=true, to_apply=%region_1.2 | all-reduce | flops 2 | bytes 16 | tf_op jit(solution)/shard_map/psum | solution.py:38
  294.9 2.0 bitcast_subtract_fusion
  296.9 14.6 %convolution_convert_fusion = bf16[384,3584]{1,0:T(8,128)(2,1)} fusion(bf16[2560,3584]{0,1:T(8,128)(2,1)} %all-gather.2.cloned.1.call-done, bf16[384,64]{0,1:T(8,128)(2,1)S(1)} %fusion.13, f32[64,2560]{1,0:T(8,128)} %bitcast_subtract_fusion, bf16[1,384,2560]{2,1,0:T(8,128)(2,1)} %param.9, pred[384]{0:T(512)(128)(4,1)S(1)} %iota_compare_fusion), kind=kOutput, calls=%fused_computation.4 | convolution fusion | flops 7183630336 | bytes 23773568 | tf_op jit(solution)/shard_map/dot_general | solution.py:29
  311.5 0.0 all-reduce.7.cloned.1.call-update
  311.5 80.5 %all-reduce.7.cloned.1.call-done = bf16[384,3584]{1,0:T(8,128)(2,1)} async-done(((bf16[384,3584]{1,0:T(8,128)(2,1)}), bf16[384,3584]{1,0:T(8,128)(2,1)}) %all-reduce.7.cloned.1.call-update) | async-done | bytes 2752528 | tf_op jit(solution)/shard_map/psum | solution.py:30
  392.1 14.7 %multiply_reduce_fusion = (f32[]{:T(128)}, f32[]{:T(128)}, f32[64,2560]{1,0:T(8,128)}) fusion(f32[64,2560]{1,0:T(8,128)} %bitcast_subtract_fusion, f32[]{:T(128)} %bitcast.72, f32[]{:T(128)S(6)} %convert_element_type.54, bf16[384,64]{0,1:T(8,128)(2,1)S(1)} %fusion.13, bf16[384,3584]{1,0:T(8,128)(2,1)} %all-reduce.7.cloned.1.call-done, ...), kind=kOutput, calls=%fused_computation.38 | convolution fusion | flops 7183237120 | bytes 24428944 | tf_op jit(solution)/shard_map/dot_general | solution.py:32
  406.8 9.5 %all-reduce = (f32[]{:T(128)}, f32[]{:T(128)}) all-reduce(f32[]{:T(128)} %get-tuple-element.3, f32[]{:T(128)} %get-tuple-element.2), channel_id=1, replica_groups=mesh['task'=8,'tp'=4] {'tp'}, use_global_device_ids=true, to_apply=%region_6.7 | all-reduce | flops 2 | bytes 16 | tf_op jit(solution)/shard_map/psum | solution.py:38
  420.5 2.7 subtract_bitcast_fusion
  (1 shorter events, 0.0 us)
Async XLA Ops:
  7.2 1.8 copy-start
  7.2 169.2 %copy-start.1 = (f32[1,64,2560]{2,1,0:T(8,128)S(1)}, f32[1,64,2560]{2,1,0:T(8,128)}, u32[]{:S(2)}) copy-start(f32[1,64,2560]{2,1,0:T(8,128)} %param.13) | copy-start | bytes 1966084
  7.2 169.2 %all-gather.2.cloned.1.call-start = ((), (), s32[]{:S(2)}) async-start(), calls=%async_computation | async-start | bytes 20643840 | tf_op jit(solution)/shard_map/all_gather | solution.py:10
  7.9 261.6 %all-reduce.5.cloned.1.call-start = ((), (), s32[]{:S(2)}) async-start(), calls=%async_computation.1 | async-start | bytes 5505024 | tf_op jit(solution)/shard_map/psum | solution.py:30
  190.8 201.3 %all-reduce.7.cloned.1.call-start = ((), (), s32[]{:S(2)}) async-start(), calls=%async_computation.2 | async-start | bytes 5505024 | tf_op jit(solution)/shard_map/psum | solution.py:30
Sparse Core Ops, SparseCore 0:
  9.6 166.6 all-gather.1
  190.9 78.5 all-reduce.4
  311.6 80.3 all-reduce.6
where the time goes:
time: 430 us
  waiting for transfers between devices  325 us (76%)
  matrix products  60 us (14%)
  between operations  20.8 us (5%)
  blocking collectives  19.3 us (4%)
  other arithmetic  4.75 us (1%)
    all_gather x1, waiting for transfers between devices, shards(): down_full = lax.all_gather(down_w, 'task', axis=1, tiled=True)  165 us
    psum x2, waiting for transfers between devices, apply(): mixed = lax.psum(partial_sum.astype(jnp.bfloat16), 'tp')  159 us
    dot_general x2, matrix products, apply(): lax.dot_general(features, second, (((0,), (0,)), ((), ())), preferred_ele...  29 us
    dot_general x2, matrix products, apply(): partial_sum = jnp.dot(active, down_full, preferred_element_type=jnp.float32)  29 us
    psum x2, blocking collectives, paired_sums(): return lax.psum((jnp.sum(vector * vector), jnp.sum(vector * image)), 'tp')  19.3 us
  transfers between devices with their start and end apart: 3, of which 3 were waited for; matrix products, arithmetic and copies ran while one was open for 0% of the time, Pallas kernels for 0%

commit v1 on v0

--- a/solution.py
+++ b/solution.py
@@ -24,10 +24,15 @@
         )
 
     def apply(vector):
+
+        def compute_goods(load):
+            ready = jnp.sum(jax.lax.all_gather(load, "tp"), axis=0)
+            return ready
+
         inner = jnp.dot(features, vector.astype(jnp.bfloat16), preferred_element_type=jnp.float32)
         active = (gated * inner).astype(jnp.bfloat16)
         partial_sum = jnp.dot(active, down_full, preferred_element_type=jnp.float32)
-        mixed = lax.psum(partial_sum.astype(jnp.bfloat16), "tp")
+        mixed = compute_goods(partial_sum.astype(jnp.bfloat16))
         second = (gated * transposed(mixed)).astype(jnp.bfloat16)
         product = lax.dot_general(
             features, second, (((0,), (0,)), ((), ())), preferred_element_type=jnp.float32

time: 430 us -> 505 us (1.17)
  waiting for transfers between devices: 325 us -> 383 us
  other arithmetic: 4.75 us -> 21.1 us
    all_gather x0 -> x2, waiting for transfers between devices: none -> 216 us  [compute_goods(): ready = jnp.sum(jax.lax.all_gather(load, 'tp'), axis=0)]
    psum x2 -> x0, waiting for transfers between devices: 159 us -> none  [apply(): mixed = lax.psum(partial_sum.astype(jnp.bfloat16), 'tp')]
    reduce_sum x0 -> x2, other arithmetic: none -> 16.3 us  [compute_goods(): ready = jnp.sum(jax.lax.all_gather(load, 'tp'), axis=0)]
where the time goes in v1:
time: 505 us
  waiting for transfers between devices  383 us (76%)
  matrix products  60.5 us (12%)
  other arithmetic  21.1 us (4%)
  between operations  21.1 us (4%)
  blocking collectives  19.4 us (4%)
    all_gather x2, waiting for transfers between devices, compute_goods(): ready = jnp.sum(jax.lax.all_gather(load, 'tp'), axis=0)  216 us
    all_gather x1, waiting for transfers between devices, shards(): down_full = lax.all_gather(down_w, 'task', axis=1, tiled=True)  165 us
    dot_general x2, matrix products, apply(): lax.dot_general(features, second, (((0,), (0,)), ((), ())), preferred_ele...  29.5 us
    dot_general x2, matrix products, apply(): partial_sum = jnp.dot(active, down_full, preferred_element_type=jnp.float32)  29.1 us
    psum x2, blocking collectives, paired_sums(): return lax.psum((jnp.sum(vector * vector), jnp.sum(vector * image)), 'tp')  19.4 us
    reduce_sum x2, other arithmetic, compute_goods(): ready = jnp.sum(jax.lax.all_gather(load, 'tp'), axis=0)  16.3 us
  transfers between devices with their start and end apart: 3, of which 3 were waited for; matrix products, arithmetic and copies ran while one was open for 0% of the time, Pallas kernels for 0%

profile of v1, /device:TPU:0, one launch (start us, length us, event | category | flops | bytes accessed | tf_op | source)
XLA Modules:
  0.0 504.8 jit_solution(14668250362427639205)
XLA Ops:
  7.2 0.0 copy-start
  7.2 0.0 copy-start.1
  7.2 0.0 all-gather.6.cloned.1.call-start
  7.2 0.7 all-gather.6.cloned.1.call-update
  7.9 0.0 all-gather.8.cloned.1.call-start
  8.9 0.1 copy-done
  8.9 2.0 fusion.13
  10.9 165.4 %all-gather.6.cloned.1.call-done = bf16[2560,3584]{0,1:T(8,128)(2,1)} async-done(((bf16[2560,448]{0,1:T(8,128)(2,1)}), bf16[2560,3584]{0,1:T(8,128)(2,1)}) %all-gather.6.cloned.1.call-update) | async-done | bytes 18350096 | tf_op jit(solution)/shard_map/all_gather | solution.py:10
  176.4 0.0 copy-done.1
  176.4 14.4 %convolution_convert_fusion.1 = bf16[384,3584]{1,0:T(8,128)(2,1)} fusion(bf16[2560,3584]{0,1:T(8,128)(2,1)} %all-gather.6.cloned.1.call-done, bf16[384,64]{0,1:T(8,128)(2,1)S(1)} %fusion.13, f32[1,64,2560]{2,1,0:T(8,128)S(1)} %copy-done.1, bf16[1,384,2560]{2,1,0:T(8,128)(2,1)} %param.9, pred[384]{0:T(512)(128)(4,1)S(1)} %iota_compare_fusion), kind=kOutput, calls=%fused_computation.5 | convolution fusion | flops 7183466496 | bytes 23773568 | tf_op jit(solution)/shard_map/dot_general | solution.py:34
  190.8 0.0 all-gather.8.cloned.1.call-update
  190.8 0.0 all-gather.10.cloned.1.call-start
  191.5 106.9 %all-gather.8.cloned.1.call-done = bf16[1536,3584]{1,0:T(8,128)(2,1)} async-done(((bf16[384,3584]{1,0:T(8,128)(2,1)}), bf16[1536,3584]{1,0:T(8,128)(2,1)}) %all-gather.8.cloned.1.call-update) | async-done | bytes 11010064 | tf_op jit(solution)/shard_map/all_gather | solution.py:29
  298.5 8.2 %reduce_sum.61 = bf16[384,3584]{1,0:T(8,128)(2,1)} reduce(bf16[4,384,3584]{2,1,0:T(8,128)(2,1)} %bitcast.75, bf16[]{:T(256)} %constant.7.clone.1), dimensions={0}, to_apply=%region_2.3 | reduce | flops 4128768 | bytes 13762562 | tf_op jit(solution)/shard_map/reduce_sum | solution.py:29
  306.6 14.5 %fusion.17 = (f32[]{:T(128)}, f32[]{:T(128)}, f32[64,2560]{1,0:T(8,128)}) fusion(f32[1,64,2560]{2,1,0:T(8,128)S(1)} %copy-done.1, f32[]{:T(128)} %bitcast.73, f32[]{:T(128)S(6)} %convert_element_type.58, bf16[384,64]{0,1:T(8,128)(2,1)S(1)} %fusion.13, bf16[384,3584]{1,0:T(8,128)(2,1)} %reduce_sum.61, bf16[2560,3584]{0,1:T(8,128)(2,1)} %all-gather.6.cloned.1.call-done, ...), kind=kOutput, calls=%fused_computation.32 | convolution fusion | flops 7183237120 | bytes 24428944 | tf_op jit(solution)/shard_map/dot_general | solution.py:37
  321.1 9.8 %all-reduce.1 = (f32[]{:T(128)}, f32[]{:T(128)}) all-reduce(f32[]{:T(128)} %get-tuple-element.5, f32[]{:T(128)} %get-tuple-element.4), channel_id=1, replica_groups=mesh['task'=8,'tp'=4] {'tp'}, use_global_device_ids=true, to_apply=%region_1.2 | all-reduce | flops 2 | bytes 16 | tf_op jit(solution)/shard_map/psum | solution.py:43
  332.2 2.0 bitcast_subtract_fusion
  334.2 14.6 %convolution_convert_fusion = bf16[384,3584]{1,0:T(8,128)(2,1)} fusion(bf16[2560,3584]{0,1:T(8,128)(2,1)} %all-gather.6.cloned.1.call-done, bf16[384,64]{0,1:T(8,128)(2,1)S(1)} %fusion.13, f32[64,2560]{1,0:T(8,128)} %bitcast_subtract_fusion, bf16[1,384,2560]{2,1,0:T(8,128)(2,1)} %param.9, pred[384]{0:T(512)(128)(4,1)S(1)} %iota_compare_fusion), kind=kOutput, calls=%fused_computation.4 | convolution fusion | flops 7183630336 | bytes 23773568 | tf_op jit(solution)/shard_map/dot_general | solution.py:34
  348.8 0.0 all-gather.10.cloned.1.call-update
  348.9 109.4 %all-gather.10.cloned.1.call-done = bf16[1536,3584]{1,0:T(8,128)(2,1)} async-done(((bf16[384,3584]{1,0:T(8,128)(2,1)}), bf16[1536,3584]{1,0:T(8,128)(2,1)}) %all-gather.10.cloned.1.call-update) | async-done | bytes 11010064 | tf_op jit(solution)/shard_map/all_gather | solution.py:29
  458.3 8.2 %reduce_sum.64 = bf16[384,3584]{1,0:T(8,128)(2,1)} reduce(bf16[4,384,3584]{2,1,0:T(8,128)(2,1)} %bitcast.76, bf16[]{:T(256)} %constant.7.clone.1), dimensions={0}, to_apply=%region_7.8 | reduce | flops 4128768 | bytes 13762562 | tf_op jit(solution)/shard_map/reduce_sum | solution.py:29
  466.4 15.0 %multiply_reduce_fusion = (f32[]{:T(128)}, f32[]{:T(128)}, f32[64,2560]{1,0:T(8,128)}) fusion(f32[64,2560]{1,0:T(8,128)} %bitcast_subtract_fusion, f32[]{:T(128)} %bitcast.74, f32[]{:T(128)S(6)} %convert_element_type.58, bf16[384,64]{0,1:T(8,128)(2,1)S(1)} %fusion.13, bf16[384,3584]{1,0:T(8,128)(2,1)} %reduce_sum.64, ...), kind=kOutput, calls=%fused_computation.38 | convolution fusion | flops 7183237120 | bytes 24428944 | tf_op jit(solution)/shard_map/dot_general | solution.py:37
  481.4 9.6 %all-reduce = (f32[]{:T(128)}, f32[]{:T(128)}) all-reduce(f32[]{:T(128)} %get-tuple-element.3, f32[]{:T(128)} %get-tuple-element.2), channel_id=1, replica_groups=mesh['task'=8,'tp'=4] {'tp'}, use_global_device_ids=true, to_apply=%region_6.7 | all-reduce | flops 2 | bytes 16 | tf_op jit(solution)/shard_map/psum | solution.py:43
  495.5 2.7 subtract_bitcast_fusion
  (1 shorter events, 0.0 us)
Async XLA Ops:
  7.2 1.8 copy-start
  7.2 169.2 %copy-start.1 = (f32[1,64,2560]{2,1,0:T(8,128)S(1)}, f32[1,64,2560]{2,1,0:T(8,128)}, u32[]{:S(2)}) copy-start(f32[1,64,2560]{2,1,0:T(8,128)} %param.13) | copy-start | bytes 1966084
  7.2 169.2 %all-gather.6.cloned.1.call-start = ((), (), s32[]{:S(2)}) async-start(), calls=%async_computation | async-start | bytes 20643840 | tf_op jit(solution)/shard_map/all_gather | solution.py:10
  7.9 290.5 %all-gather.8.cloned.1.call-start = ((), (), s32[]{:S(2)}) async-start(), calls=%async_computation.1 | async-start | bytes 13762560 | tf_op jit(solution)/shard_map/all_gather | solution.py:29
  190.8 267.5 %all-gather.10.cloned.1.call-start = ((), (), s32[]{:S(2)}) async-start(), calls=%async_computation.2 | async-start | bytes 13762560 | tf_op jit(solution)/shard_map/all_gather | solution.py:29
Sparse Core Ops, SparseCore 0:
  9.6 166.6 all-gather.5
  190.9 107.4 all-gather.7
  349.0 109.2 all-gather.9
